TPU v7x, 32 devices: a whole 2x2x4 slice. The times are simulated.
32 devices in a mesh: seq: 16 (over z, y, x), tensor: 2 (over core).
Axes of the slice: x: 2, y: 2, z: 4, core: 2. Of those that a mesh axis runs over, the one named last changes fastest.
Arguments:
- hidden: bfloat16 [2, 4096, 8192], P(None, 'seq', 'tensor'), may hold values from -160 to 160
- norm_gain: bfloat16 [8192], P('tensor'), may hold values from 0.25 to 1.75
- value_weight: bfloat16 [8192], P('tensor'), may hold values from -0.0625 to 0.0625
- rewards: float32 [2, 4096], P(None, 'seq'), may hold values from -6 to 6
- done_flags: int32 [2, 4096], P(None, 'seq'), may hold values 0 or 1
- valid_mask: int32 [2, 4096], P('tensor', 'seq'), may hold values 0 or 1
- new_logprob: float32 [2, 4096], P('tensor', 'seq'), may hold values from -1 to 1
- old_logprob: float32 [2, 4096], P('tensor', 'seq'), may hold values from -1 to 1
- discount: float32 [2], replicated, may hold values from 0.9 to 1
- trace_decay: float32 [2], replicated, may hold values from 0.9 to 1
- bootstrap: float32 [2], replicated, may hold values from -5 to 5
Outputs:
- values: float32 [2, 4096], P('tensor', 'seq')
- white_adv: float32 [2, 4096], P('tensor', 'seq')
- token_loss: float32 [2, 4096], P('tensor', 'seq')
- policy_loss: float32 [], replicated
All inputs are finite; a program needn't handle non-finite values. No bound on the sum of `done_flags` or of `valid_mask` on one device may be relied on, other than what follows from the above.
Results may differ from a plain program's by a relative error of at most 0.00035.
Values sent between devices are 32-bit elements; how exact they have to be, the bound alone decides.
A program may use at most 64 MiB of HBM per device.

v0:
```python
import jax
import jax.numpy as jnp
from jax import lax
from jax.sharding import PartitionSpec as P

H = 8192


EPS_NORM = 1e-06
EPS_WHITE = 1e-08
CLIP = 0.2
HIGHEST = lax.Precision.HIGHEST


def compose(earlier, later):
    return (later[0] + later[1] * earlier[0], later[1] * earlier[1])


def local_pass(values, rewards, done_flags, discount, trace_decay):
    row_count, length = values.shape
    alive = 1.0 - done_flags.astype(jnp.float32)
    inner_next = jnp.concatenate([values[:, 1:], jnp.zeros((row_count, 1), jnp.float32)], axis=1)
    delta = rewards + discount[:, None] * alive * inner_next - values
    decay = discount * trace_decay
    counted = jnp.cumsum(done_flags, axis=1) - done_flags
    later_pos = lax.broadcasted_iota(jnp.int32, (length, length), 1)
    early_pos = lax.broadcasted_iota(jnp.int32, (length, length), 0)
    upper = later_pos >= early_pos
    distance = jnp.maximum(later_pos - early_pos, 0).astype(jnp.float32)
    powers = jnp.exp(distance[None, :, :] * jnp.log(decay)[:, None, None])
    same_episode = counted[:, None, :] == counted[:, :, None]
    weights = jnp.where(upper[None, :, :] & same_episode, powers, 0.0)
    local_adv = jnp.einsum(
        "stj,sj->st", weights, delta, precision=HIGHEST, preferred_element_type=jnp.float32
    )
    coef = weights[:, :, length - 1] * (discount * alive[:, length - 1])[:, None]
    return (local_adv, coef)


def fold_step(carry, block):
    return (compose(carry, block), carry)


def shards(
    hidden,
    norm_gain,
    value_weight,
    rewards,
    done_flags,
    valid_mask,
    new_logprob,
    old_logprob,
    discount,
    trace_decay,
    bootstrap,
):
    seqs_all = hidden.shape[0]
    own_rows = seqs_all // lax.axis_size("tensor")
    first_row = lax.axis_index("tensor") * own_rows
    scaled = norm_gain.astype(jnp.float32) * value_weight.astype(jnp.float32)
    squares = jnp.einsum("sth,sth->st", hidden, hidden, preferred_element_type=jnp.float32)
    products = jnp.einsum(
        "sth,h->st", hidden, scaled, precision=HIGHEST, preferred_element_type=jnp.float32
    )
    squares, products = (
        lax.psum_scatter(squares, "tensor", scatter_dimension=0, tiled=True),
        lax.psum_scatter(products, "tensor", scatter_dimension=0, tiled=True),
    )
    values = products * lax.rsqrt(squares / H + EPS_NORM)

    def pick(array):
        return lax.dynamic_slice_in_dim(array, first_row, own_rows, 0)

    rewards_rows = pick(rewards)
    flags_rows = pick(done_flags)
    discount_rows = pick(discount)
    trace_rows = pick(trace_decay)
    local_adv, coef = local_pass(values, rewards_rows, flags_rows, discount_rows, trace_rows)
    weight = valid_mask.astype(jnp.float32)
    offset = values[:, 0] + trace_rows * local_adv[:, 0]
    slope = trace_rows * coef[:, 0]
    packed = jnp.stack(
        [
            offset,
            slope,
            jnp.sum(weight, axis=1),
            jnp.sum(weight * local_adv, axis=1),
            jnp.sum(weight * coef, axis=1),
            jnp.sum(weight * local_adv * local_adv, axis=1),
            jnp.sum(weight * local_adv * coef, axis=1),
            jnp.sum(weight * coef * coef, axis=1),
        ],
        axis=1,
    )
    gathered = lax.all_gather(packed[None], ("seq", "tensor"), axis=0, tiled=True)
    seq_count = lax.axis_size("seq")
    table = gathered.reshape(seq_count, seqs_all, 8)
    start_pair = (jnp.zeros((seqs_all,), jnp.float32), jnp.ones((seqs_all,), jnp.float32))
    _, prefix = lax.scan(fold_step, start_pair, (table[:, :, 0], table[:, :, 1]), reverse=True)
    entering = prefix[0] + prefix[1] * bootstrap[None, :]
    count = jnp.sum(table[:, :, 2])
    total = jnp.sum(table[:, :, 3] + entering * table[:, :, 4])
    square_sum = jnp.sum(
        table[:, :, 5] + 2.0 * entering * table[:, :, 6] + entering * entering * table[:, :, 7]
    )
    mean = total / count
    variance = square_sum / count - mean * mean
    own_entering = lax.dynamic_slice_in_dim(
        lax.dynamic_index_in_dim(entering, lax.axis_index("seq"), 0, False), first_row, own_rows, 0
    )
    adv_own = local_adv + coef * own_entering[:, None]
    white_adv = (adv_own - mean) * lax.rsqrt(variance + EPS_WHITE)
    ratio = jnp.exp(new_logprob - old_logprob)
    surrogate = jnp.minimum(ratio * white_adv, jnp.clip(ratio, 1.0 - CLIP, 1.0 + CLIP) * white_adv)
    token_loss = -weight * surrogate
    loss_sum = lax.psum(jnp.sum(token_loss), ("seq", "tensor"))
    policy_loss = loss_sum / count
    return (values, white_adv, token_loss, policy_loss)


def solution(mesh):
    in_specs = (
        P(None, "seq", "tensor"),
        P("tensor"),
        P("tensor"),
        P(None, "seq"),
        P(None, "seq"),
        P("tensor", "seq"),
        P("tensor", "seq"),
        P("tensor", "seq"),
        P(),
        P(),
        P(),
    )
    out_specs = (P("tensor", "seq"), P("tensor", "seq"), P("tensor", "seq"), P())
    return jax.shard_map(shards, mesh=mesh, in_specs=in_specs, out_specs=out_specs, check_vma=False)
```

profile of v0, /device:TPU:0, one launch (start us, length us, event | category | flops | bytes accessed | tf_op | source)
XLA Modules:
  0.0 121.4 jit_solution(13526523173218547624)
XLA Ops:
  0.6 0.0 copy-start
  0.6 0.9 convert_multiply_fusion.1
  1.5 0.0 copy-start.10
  1.5 0.0 copy-start.3
  1.5 0.0 copy-start.8
  1.6 0.0 copy-start.7
  1.6 0.0 copy-start.4
  1.6 0.0 copy-start.5
  1.6 6.0 %fusion.45 = f32[1,2,256]{2,0,1:T(1,128)S(1)} fusion(f32[4096,1,1]{0,1,2:T(1,128)S(1)} %bitcast.83, bf16[2,256,4096]{2,1,0:T(8,128)(2,1)} %param.13), kind=kOutput, calls=%fused_computation.75 | convolution fusion | flops 25165824 | bytes 4212736 | tf_op jit(solution)/shard_map/sth,h->st/dot_general | solution.py:62
  7.6 0.9 fusion.3
  8.5 2.6 %all-reduce.2 = (f32[2,256]{1,0:T(2,128)S(1)}, f32[2,256]{1,0:T(2,128)S(1)}) all-reduce(f32[2,256]{1,0:T(2,128)S(1)} %bitcast.85, f32[2,256]{1,0:T(2,128)S(1)} %fusion.3), channel_id=3, replica_groups=mesh['seq'=16,'tensor'=2] {'tensor'}, use_global_device_ids=true, to_apply=%region_0.0.clone | all-reduce | flops 1024 | bytes 8192
  11.1 0.6 dynamic-slice.1
  11.7 0.7 dynamic-slice_multiply_fusion.1
  12.4 0.0 copy-start.1
  12.4 0.6 dynamic_slice.37
  13.0 0.6 slice.66
  14.9 0.6 dynamic_slice.38
  16.8 0.3 reduce-window.6
  17.1 0.2 slice_reduce_fusion.1
  17.3 0.2 reduce-window.9
  17.5 0.1 broadcast.116
  17.6 0.6 slice.65
  18.1 0.1 slice.64
  18.2 2.3 %multiply_reduce_fusion = (f32[]{:T(128)}, f32[]{:T(128)}, f32[]{:T(128)}, f32[]{:T(128)}, f32[]{:T(128)}, /*index=5*/f32[]{:T(128)}, f32[1,256,1]{1,2,0:T(1,128)S(1)}, f32[1,256]{1,0:T(1,128)S(1)}) fusion(s32[1,256]{1,0:T(1,128)S(1)} %copy-done.3, f32[]{:T(128)} %bitcast.13, f32[]{:T(128)} %bitcast.7, s32[256]{0:T(256)S(1)} %bitcast.96, s32[1]{0:T(128)} %slice.65, ...), kind=kOutput, calls=%fused_computation.56 | convolution fusion | flops 1318138 | bytes 13340 | tf_op jit(solution)/shard_map/stj,sj->st/dot_general | solution.py:33
  20.5 0.5 slice.67
  21.1 0.5 slice.68
  23.5 0.5 slice.69
  25.3 3.8 %stack.35 = f32[1,8]{1,0:T(1,128)S(1)} concatenate(f32[1,1]{1,0:T(1,128)} %bitcast.16, f32[1,1]{1,0:T(1,128)} %bitcast.19, f32[1,1]{1,0:T(1,128)} %bitcast.20, f32[1,1]{1,0:T(1,128)} %bitcast.21, f32[1,1]{1,0:T(1,128)} %bitcast.22, f32[1,1]{1,0:T(1,128)} %bitcast.23, f32[1,1]{1,0:T(1,128)} %bitcast.24, f32[1,1]{1,0:T(1,128)} %bitcast.25), dimensions={1} | concatenate | bytes 64 | tf_op jit(solution)/shard_map/stack | solution.py:82
  29.2 43.1 %all-gather.1 = f32[32,1,8]{2,1,0:T(1,128)S(1)} all-gather(f32[1,1,8]{2,1,0:T(1,128)S(1)} %bitcast.92), channel_id=2, replica_groups=mesh['seq'=16,'tensor'=2] {'seq','tensor'}, dimensions={0}, use_global_device_ids=true | all-gather | bytes 1056 | tf_op jit(solution)/shard_map/all_gather | solution.py:95
  72.3 0.7 slice_reduce_fusion
  73.0 0.1 copy.56
  73.1 0.1 copy.55
  73.2 0.1 copy.59
  73.3 0.1 copy.58
  73.3 0.1 copy.57
  73.4 0.1 copy.53
  73.5 0.1 copy.39
  73.6 0.1 copy.54
  73.7 0.1 copy.40
  73.8 1.9 %while.21 = (s32[]{:T(128)}, f32[2]{0:T(128)S(1)}, f32[2]{0:T(128)S(1)}, f32[16,2]{1,0:T(8,128)S(1)}, f32[16,2]{1,0:T(8,128)S(1)}, /*index=5*/f32[16,2]{1,0:T(8,...) while((s32[]{:T(128)}, f32[2]{0:T(128)S(1)}, f32[2]{0:T(128)S(1)}, ...), condition=%wide.region_11.12_spmd.clone, body=%wide.region_10.11_spmd.clone.sunk | while | flops 14 | bytes 239 | solution.py:99
  75.7 0.1 copy.42
  75.8 0.1 copy.41
  75.9 0.7 fusion.34
  76.5 0.7 dynamic_slice.40
  77.2 0.7 broadcast_multiply_fusion
  80.6 0.0 copy-start.2
  80.7 1.3 %fusion.43 = (f32[]{:T(128)}, f32[1,256]{1,0:T(1,128)}) fusion(f32[1,256]{1,0:T(1,128)S(1)} %bitcast.90, f32[1,256]{1,0:T(1,128)S(1)} %copy-done.4, f32[1,256]{1,0:T(1,128)S(1)} %copy-done.5, s32[1,256]{1,0:T(1,128)S(1)} %copy-done.3), kind=kLoop, calls=%fused_computation.74 | loop fusion | flops 2303 | bytes 5124 | tf_op jit(solution)/shard_map/reduce_sum | solution.py:116
  81.9 37.0 %psum.7 = f32[]{:T(128)} all-reduce(f32[]{:T(128)} %get-tuple-element.217), channel_id=1, replica_groups=mesh['seq'=16,'tensor'=2] {'seq','tensor'}, use_global_device_ids=true, to_apply=%region_16.17 | all-reduce | flops 1 | bytes 8 | tf_op jit(solution)/shard_map/psum | solution.py:116
  (72 shorter events, 1.6 us)
Async XLA Ops:
  0.6 6.9 %copy-start = (bf16[2,256,4096]{2,1,0:T(8,128)(2,1)S(1)}, bf16[2,256,4096]{2,1,0:T(8,128)(2,1)}, u32[]{:S(2)}) copy-start(bf16[2,256,4096]{2,1,0:T(8,128)(2,1)} %param.13) | copy-start | bytes 12582916
  1.5 9.6 %copy-start.11 = (u32[32]{0:T(128)S(1)}, u32[32]{0:T(128)}, u32[]{:S(2)}) copy-start(u32[32]{0:T(128)} %constant.101) | copy-start | bytes 388
  1.5 10.9 %copy-start.9 = (f32[2]{0:T(128)S(1)}, f32[2]{0:T(128)}, u32[]{:S(2)}) copy-start(f32[2]{0:T(128)} %param.21) | copy-start | bytes 28
  1.5 11.5 %copy-start.6 = (s32[2,256]{1,0:T(2,128)S(1)}, s32[2,256]{1,0:T(2,128)}, u32[]{:S(2)}) copy-start(s32[2,256]{1,0:T(2,128)} %param.17) | copy-start | bytes 6148
  1.5 13.3 %copy-start.10 = (f32[2]{0:T(128)S(1)}, f32[2]{0:T(128)}, u32[]{:S(2)}) copy-start(f32[2]{0:T(128)} %param.22) | copy-start | bytes 28
  1.5 16.7 %copy-start.3 = (s32[1,256]{1,0:T(1,128)S(1)}, s32[1,256]{1,0:T(1,128)}, u32[]{:S(2)}) copy-start(s32[1,256]{1,0:T(1,128)} %param.18) | copy-start | bytes 3076
  1.5 16.7 %copy-start.8 = (f32[2,256]{1,0:T(2,128)S(1)}, f32[2,256]{1,0:T(2,128)}, u32[]{:S(2)}) copy-start(f32[2,256]{1,0:T(2,128)} %param.16) | copy-start | bytes 6148
  1.6 74.3 %copy-start.7 = (f32[2]{0:T(128)S(1)}, f32[2]{0:T(128)}, u32[]{:S(2)}) copy-start(f32[2]{0:T(128)} %param.23) | copy-start | bytes 28
  1.6 79.1 %copy-start.4 = (f32[1,256]{1,0:T(1,128)S(1)}, f32[1,256]{1,0:T(1,128)}, u32[]{:S(2)}) copy-start(f32[1,256]{1,0:T(1,128)} %param.19) | copy-start | bytes 3076
  1.6 79.1 %copy-start.5 = (f32[1,256]{1,0:T(1,128)S(1)}, f32[1,256]{1,0:T(1,128)}, u32[]{:S(2)}) copy-start(f32[1,256]{1,0:T(1,128)} %param.20) | copy-start | bytes 3076
  12.4 107.9 %copy-start.1 = (f32[1,256]{1,0:T(1,128)}, f32[1,256]{1,0:T(1,128)S(1)}, u32[]{:S(2)}) copy-start(f32[1,256]{1,0:T(1,128)S(1)} %dynamic-slice_multiply_fusion.1) | copy-start | bytes 3076
  80.6 39.6 %copy-start.2 = (f32[256]{0:T(256)}, f32[256]{0:T(256)S(1)}, u32[]{:S(2)}) copy-start(f32[256]{0:T(256)S(1)} %subtract_multiply_fusion) | copy-start | bytes 3076
where the time goes:
time: 123 us; the launch traced here: 121 us
  blocking collectives  82.8 us (67%)
  between operations  11.8 us (10%)
  local copies, waits for them, and re-layouts  11.5 us (9%)
  matrix products  8.29 us (7%)
  other arithmetic  6.61 us (5%)
    all_gather x1, blocking collectives, shards(): lax.all_gather(packed[None], ('seq', 'tensor'), axis=0, tiled=True)  43.1 us
    psum x1, blocking collectives, shards(): loss_sum = lax.psum(jnp.sum(token_loss), ('seq', 'tensor'))  37 us
    dot_general x1, matrix products, shards(): jnp.einsum('sth,h->st', hidden, scaled, precision=HIGHEST, preferred_elem...  5.97 us
    another operation x1, local copies, waits for them, and re-layouts, shards(): jnp.stack([offset, slope, jnp.sum(weight, axis=1), jnp.sum(weight * local...  3.84 us
    unnamed x1, blocking collectives  2.63 us

commit v1 on v0

v1 whole, which is shorter than its diff:
```python
import functools

import jax
import jax.numpy as jnp
from jax import lax
from jax.experimental import pallas as pl
from jax.experimental.pallas import tpu as pltpu
from jax.sharding import PartitionSpec as P

EPS_NORM = 1e-06
EPS_WHITE = 1e-08
CLIP = 0.2
HIGHEST = lax.Precision.HIGHEST
LANES = 128
BLOCK = 32


def lane_sums(parts):
    ones = jnp.ones((8, LANES), jnp.float32)
    return lax.dot_general(
        ones, parts, (((1,), (1,)), ((), ())), precision=HIGHEST, preferred_element_type=jnp.float32
    )


def kernel(
    seq_count,
    tensor_count,
    width,
    chunk,
    hidden_hbm,
    gain_hbm,
    weight_hbm,
    rewards_hbm,
    flags_hbm,
    mask_hbm,
    new_hbm,
    old_hbm,
    discount_hbm,
    trace_hbm,
    boot_hbm,
    values_ref,
    white_ref,
    token_ref,
    loss_ref,
    hid,
    gain,
    wgt,
    rew,
    flg,
    msk,
    newp,
    oldp,
    disc,
    trc,
    boot,
    scaled,
    parts,
    part_send,
    part_recv,
    early,
    late,
    carry,
    hid_sem,
    in_sem,
    part_send_sem,
    part_recv_sem,
    early_send_sem,
    early_recv_sem,
    late_send_sem,
    late_recv_sem,
):
    seqs_all, length, local_width = hid.shape
    own_rows = seqs_all // tensor_count
    devices = seq_count * tensor_count
    chunks = length // chunk
    me_seq = lax.axis_index("seq")
    me_ten = lax.axis_index("tensor")
    first_row = me_ten * own_rows
    my_slot = me_ten * seq_count + me_seq

    small = [
        (gain_hbm, gain),
        (weight_hbm, wgt),
        (rewards_hbm, rew),
        (flags_hbm, flg),
        (mask_hbm, msk),
        (new_hbm, newp),
        (old_hbm, oldp),
        (discount_hbm, disc),
        (trace_hbm, trc),
        (boot_hbm, boot),
    ]
    small_copies = [
        pltpu.make_async_copy(src, dst, in_sem.at[i]) for i, (src, dst) in enumerate(small)
    ]
    for copy in small_copies:
        copy.start()

    def hid_copy(i, c):
        row = lax.rem(first_row + own_rows + i, seqs_all)
        rows = pl.ds(pl.multiple_of(c * chunk, chunk), chunk)
        return pltpu.make_async_copy(
            hidden_hbm.at[row, rows, :], hid.at[i, rows, :], hid_sem.at[i * chunks + c]
        )

    for i in range(seqs_all):
        for c in range(chunks):
            hid_copy(i, c).start()

    barrier = pltpu.get_barrier_semaphore()

    def peer(k):
        slot = lax.rem(my_slot + k, devices)
        return (lax.rem(slot, seq_count), lax.div(slot, seq_count))

    def greet(k, _):
        pl.semaphore_signal(
            barrier, inc=1, device_id=peer(k), device_id_type=pl.DeviceIdType.MESH
        )
        return 0

    lax.fori_loop(1, devices, greet, 0)

    for copy in small_copies:
        copy.wait()

    for j in range(local_width // LANES):
        cols = pl.ds(j * LANES, LANES)
        row = gain[0:1, cols].astype(jnp.float32) * wgt[0:1, cols].astype(jnp.float32)
        scaled[:, cols] = jnp.broadcast_to(row, (8, LANES))

    lane = lax.broadcasted_iota(jnp.int32, (8, length), 1)
    steps = []
    step = 1
    while step < length:
        steps.append(step)
        step *= 2
    ahead = lambda x, d: pltpu.roll(x, length - d, 1)
    rows_info = []
    for r in range(own_rows):
        discount = jnp.full((8, length), disc[first_row + r], jnp.float32)
        trace = jnp.full((8, length), trc[first_row + r], jnp.float32)
        flags = jnp.broadcast_to(flg[pl.ds(first_row + r, 1), :], (8, length))
        alive = 1.0 - flags.astype(jnp.float32)
        link = discount * trace * alive
        level = jnp.where(lane < length - 1, link, 0.0)
        coef = jnp.where(lane < length - 1, link, discount * alive)
        levels = []
        for d in steps:
            levels.append(level)
            level = level * ahead(level, d)
            coef = coef * jnp.where(lane < length - d, ahead(coef, d), 1.0)
        ratio = jnp.exp(newp[r : r + 1, :] - oldp[r : r + 1, :])
        weight = msk[r : r + 1, :].astype(jnp.float32)
        reward = jnp.broadcast_to(rew[pl.ds(first_row + r, 1), :], (8, length))
        following = jnp.where(lane < length - 1, discount * alive, 0.0)
        rows_info.append((trace, levels, coef, ratio, weight, reward, following))
        early[my_slot, r : r + 1, 0:length] = ratio
        early[my_slot, r : r + 1, length : 2 * length] = weight
        early[my_slot, r : r + 1, 2 * length : 3 * length] = coef[0:1, :]
        early[my_slot, r : r + 1, 3 * length : 3 * length + LANES] = jnp.broadcast_to(
            trace[0:1, 0:1] * coef[0:1, 0:1], (1, LANES)
        )

    def row_sums(i):
        def do_chunk(c, _):
            hid_copy(i, c).wait()
            for b in range(chunk // BLOCK):
                rows = pl.ds(pl.multiple_of(c * chunk + b * BLOCK, BLOCK), BLOCK)
                squares = jnp.zeros((BLOCK // 8, 8, LANES), jnp.float32)
                products = jnp.zeros((BLOCK // 8, 8, LANES), jnp.float32)
                for j in range(local_width // LANES):
                    cols = pl.ds(j * LANES, LANES)
                    x = hid[i, rows, cols].astype(jnp.float32).reshape(BLOCK // 8, 8, LANES)
                    squares = squares + x * x
                    products = products + x * scaled[:, cols][None]
                parts[0, rows, :] = squares.reshape(BLOCK, LANES)
                parts[1, rows, :] = products.reshape(BLOCK, LANES)
            return 0

        lax.fori_loop(0, chunks, do_chunk, 0)
        return lane_sums(parts[0]), lane_sums(parts[1])

    for k in range(1, tensor_count):
        for r in range(own_rows):
            squares, products = row_sums((k - 1) * own_rows + r)
            part_send[k - 1, 2 * r : 2 * r + 1, :] = squares[0:1, :]
            part_send[k - 1, 2 * r + 1 : 2 * r + 2, :] = products[0:1, :]

    pl.semaphore_wait(barrier, devices - 1)

    part_copies = []
    for k in range(1, tensor_count):
        copy = pltpu.make_async_remote_copy(
            src_ref=part_send.at[k - 1],
            dst_ref=part_recv.at[k - 1],
            send_sem=part_send_sem.at[k - 1],
            recv_sem=part_recv_sem.at[k - 1],
            device_id=(me_seq, lax.rem(me_ten + k, tensor_count)),
            device_id_type=pl.DeviceIdType.MESH,
        )
        copy.start()
        part_copies.append(copy)

    def send_all(buffer, send_sem, recv_sem):
        def send(k, _):
            pltpu.make_async_remote_copy(
                src_ref=buffer.at[my_slot],
                dst_ref=buffer.at[my_slot],
                send_sem=send_sem,
                recv_sem=recv_sem,
                device_id=peer(k),
                device_id_type=pl.DeviceIdType.MESH,
            ).start()
            return 0

        lax.fori_loop(1, devices, send, 0)

    def all_blocks(buffer, sem):
        view = buffer.at[pl.ds(0, devices - 1)]
        return pltpu.make_async_copy(view, view, sem)

    send_all(early, early_send_sem, early_recv_sem)

    own = [row_sums((tensor_count - 1) * own_rows + r) for r in range(own_rows)]
    for copy in part_copies:
        copy.wait()

    for r in range(own_rows):
        trace, levels, coef, ratio, weight, reward, following = rows_info[r]
        squares, products = own[r]
        for k in range(1, tensor_count):
            squares = squares + part_recv[k - 1, 2 * r : 2 * r + 1, :]
            products = products + part_recv[k - 1, 2 * r + 1 : 2 * r + 2, :]
        values = products * lax.rsqrt(squares / width + EPS_NORM)
        values_ref[r : r + 1, :] = values[0:1, :]
        adv = reward + following * ahead(values, 1) - values
        for d, level in zip(steps, levels):
            adv = adv + level * ahead(adv, d)
        late[my_slot, r : r + 1, 0:length] = adv[0:1, :]
        late[my_slot, r : r + 1, length : length + LANES] = jnp.broadcast_to(
            values[0:1, 0:1] + trace[0:1, 0:1] * adv[0:1, 0:1], (1, LANES)
        )

    send_all(late, late_send_sem, late_recv_sem)

    all_blocks(early, early_recv_sem).wait()
    count = jnp.zeros((seq_count, length), jnp.float32)
    for t in range(tensor_count):
        for r in range(own_rows):
            count = count + early[pl.ds(t * seq_count, seq_count), r, length : 2 * length]
    total = lambda x: jnp.sum(jnp.sum(x, axis=0, keepdims=True), axis=1, keepdims=True)
    count = total(count)
    all_blocks(late, late_recv_sem).wait()

    advs = []
    for t in range(tensor_count):
        for r in range(own_rows):
            entering = jnp.full((1, LANES), boot[t * own_rows + r], jnp.float32)
            for n in range(seq_count - 1, -1, -1):
                slot = t * seq_count + n
                carry[slot, r : r + 1, :] = entering
                if n:
                    offset = late[slot, r : r + 1, length : length + LANES]
                    slope = early[slot, r : r + 1, 3 * length : 3 * length + LANES]
                    entering = offset + slope * entering
    sums = jnp.zeros((seq_count, length), jnp.float32)
    for t in range(tensor_count):
        for r in range(own_rows):
            slots = pl.ds(t * seq_count, seq_count)
            entering = jnp.concatenate([carry[slots, r, :]] * (length // LANES), axis=1)
            adv = late[slots, r, 0:length] + early[slots, r, 2 * length : 3 * length] * entering
            advs.append(adv)
            sums = sums + early[slots, r, length : 2 * length] * adv
    mean = total(sums) / count
    sums = jnp.zeros((seq_count, length), jnp.float32)
    for t in range(tensor_count):
        for r in range(own_rows):
            slots = pl.ds(t * seq_count, seq_count)
            centred = advs[t * own_rows + r] - mean
            advs[t * own_rows + r] = centred
            sums = sums + early[slots, r, length : 2 * length] * centred * centred
    scale = lax.rsqrt(total(sums) / count + EPS_WHITE)

    def token_loss(ratio, weight, white):
        clipped = jnp.clip(ratio, 1.0 - CLIP, 1.0 + CLIP)
        return -weight * jnp.minimum(ratio * white, clipped * white)

    for r in range(own_rows):
        _, _, coef, ratio, weight, _, _ = rows_info[r]
        entering = carry[my_slot, r : r + 1, :]
        entering = jnp.concatenate([entering] * (length // LANES), axis=1)
        adv = late[my_slot, r : r + 1, 0:length] + coef[0:1, :] * entering
        white = (adv - mean) * scale
        white_ref[r : r + 1, :] = white
        token_ref[r : r + 1, :] = token_loss(ratio, weight, white)

    sums = jnp.zeros((seq_count, length), jnp.float32)
    for t in range(tensor_count):
        for r in range(own_rows):
            slots = pl.ds(t * seq_count, seq_count)
            sums = sums + token_loss(
                early[slots, r, 0:length],
                early[slots, r, length : 2 * length],
                advs[t * own_rows + r] * scale,
            )
    loss_ref[...] = total(sums) / count

    all_blocks(early, early_send_sem).wait()
    all_blocks(late, late_send_sem).wait()


def shards(seq_count, tensor_count, hidden, norm_gain, value_weight, *rest):
    seqs_all, length, local_width = hidden.shape
    own_rows = seqs_all // tensor_count
    devices = seq_count * tensor_count
    chunk = min(length, 64)
    f32 = jnp.float32
    row = jax.ShapeDtypeStruct((own_rows, length), f32)
    dma = pltpu.SemaphoreType.DMA
    outs = pl.pallas_call(
        functools.partial(kernel, seq_count, tensor_count, local_width * tensor_count, chunk),
        out_shape=[row, row, row, jax.ShapeDtypeStruct((1, 1), f32)],
        in_specs=[pl.BlockSpec(memory_space=pl.ANY)] * 11,
        out_specs=[pl.BlockSpec(memory_space=pltpu.VMEM)] * 4,
        scratch_shapes=[
            pltpu.VMEM((seqs_all, length, local_width), jnp.bfloat16),
            pltpu.VMEM((1, local_width), jnp.bfloat16),
            pltpu.VMEM((1, local_width), jnp.bfloat16),
            pltpu.VMEM((seqs_all, length), f32),
            pltpu.VMEM((seqs_all, length), jnp.int32),
            pltpu.VMEM((own_rows, length), jnp.int32),
            pltpu.VMEM((own_rows, length), f32),
            pltpu.VMEM((own_rows, length), f32),
            pltpu.SMEM((seqs_all,), f32),
            pltpu.SMEM((seqs_all,), f32),
            pltpu.SMEM((seqs_all,), f32),
            pltpu.VMEM((8, local_width), f32),
            pltpu.VMEM((2, length, LANES), f32),
            pltpu.VMEM((max(tensor_count - 1, 1), 2 * own_rows, length), f32),
            pltpu.VMEM((max(tensor_count - 1, 1), 2 * own_rows, length), f32),
            pltpu.VMEM((devices, own_rows, 3 * length + LANES), f32),
            pltpu.VMEM((devices, own_rows, length + LANES), f32),
            pltpu.VMEM((devices, own_rows, LANES), f32),
            dma((seqs_all * (length // chunk),)),
            dma((10,)),
            dma((max(tensor_count - 1, 1),)),
            dma((max(tensor_count - 1, 1),)),
            dma,
            dma,
            dma,
            dma,
        ],
        compiler_params=pltpu.CompilerParams(collective_id=0, has_side_effects=True),
    )(hidden, norm_gain.reshape(1, -1), value_weight.reshape(1, -1), *rest)
    return (outs[0], outs[1], outs[2], outs[3].reshape(()))


def solution(mesh):
    in_specs = (
        P(None, "seq", "tensor"),
        P("tensor"),
        P("tensor"),
        P(None, "seq"),
        P(None, "seq"),
        P("tensor", "seq"),
        P("tensor", "seq"),
        P("tensor", "seq"),
        P(),
        P(),
        P(),
    )
    out_specs = (P("tensor", "seq"), P("tensor", "seq"), P("tensor", "seq"), P())
    body = functools.partial(shards, mesh.shape["seq"], mesh.shape["tensor"])
    return jax.shard_map(body, mesh=mesh, in_specs=in_specs, out_specs=out_specs, check_vma=False)
```

time: 123 us -> 23.9 us (0.19); the launches traced: 121 us -> 23.5 us
  blocking collectives: 82.8 us -> 0 us
  Pallas kernels: 0 us -> 14.9 us
  between operations: 11.8 us -> 2.33 us
  matrix products: 8.29 us -> 0 us
  other arithmetic: 6.61 us -> 0 us
  local copies, waits for them, and re-layouts: 11.5 us -> 6.24 us
    all_gather x1 -> x0, blocking collectives: 43.1 us -> none  [shards(): lax.all_gather(packed[None], ('seq', 'tensor'), axis=0, tiled=True)]
    psum x1 -> x0, blocking collectives: 37 us -> none  [shards(): loss_sum = lax.psum(jnp.sum(token_loss), ('seq', 'tensor'))]
    pallas_call x0 -> x1, Pallas kernels: none -> 14.9 us  [shards(): pl.pallas_call(functools.partial(kernel, seq_count, tensor_count, local_w...]
    dot_general x2 -> x0, matrix products: 8.29 us -> none  [the longest x1 5.97 us: shards(): jnp.einsum('sth,h->st', hidden, scaled, precision=HIGHEST, preferred_elem...]
    another operation x5 -> x0, local copies, waits for them, and re-layouts: 3.92 us -> none  [the longest x1 3.84 us: shards(): jnp.stack([offset, slope, jnp.sum(weight, axis=1), jnp.sum(weight * local...]
    slice x7 -> x0, local copies, waits for them, and re-layouts: 2.96 us -> none  [the longest x2 1.02 us: shards(): offset = values[:, 0] + trace_rows * local_adv[:, 0]]
    reduce_sum x3 -> x0, other arithmetic: 2.64 us -> none  [the longest x1 1.26 us: shards(): loss_sum = lax.psum(jnp.sum(token_loss), ('seq', 'tensor'))]
    unnamed x1 -> x0, blocking collectives: 2.63 us -> none
where the time goes in v1:
time: 23.9 us; the launch traced here: 23.5 us
  Pallas kernels  14.9 us (62%)
  local copies, waits for them, and re-layouts  6.24 us (26%)
  between operations  2.33 us (10%)
    pallas_call x1, Pallas kernels, shards(): pl.pallas_call(functools.partial(kernel, seq_count, tensor_count, local_w...  14.9 us
    unnamed x3, local copies, waits for them, and re-layouts  3.62 us
    reshape x1, local copies, waits for them, and re-layouts, shards(): norm_gain.reshape(1, -1)  1.31 us
    reshape x1, local copies, waits for them, and re-layouts, shards(): value_weight.reshape(1, -1)  1.3 us

profile of v1, /device:TPU:0, one launch (start us, length us, event | category | flops | bytes accessed | tf_op | source)
XLA Modules:
  0.0 23.5 jit_solution(2128132275336502482)
XLA Ops:
  0.6 1.3 %reshape.17.gain_hbm = bf16[1,4096]{1,0:T(2,128)(2,1)} reshape(bf16[4096]{0:T(1024)(128)(2,1)} %param.12) | data formatting | bytes 16384 | tf_op jit(solution)/shard_map/reshape | solution.py:355
  1.9 1.3 %reshape.18.weight_hbm = bf16[1,4096]{1,0:T(2,128)(2,1)} reshape(bf16[4096]{0:T(1024)(128)(2,1)} %param.13) | data formatting | bytes 16384 | tf_op jit(solution)/shard_map/reshape | solution.py:355
  3.2 14.9 %shard_map.138 = (f32[1,256]{1,0:T(1,128)}, f32[1,256]{1,0:T(1,128)}, f32[1,256]{1,0:T(1,128)}, f32[1,1]{1,0:T(1,128)}) custom-call(bf16[2,256,4096]{2,1,0:T(8,128)(2,1)} %hidden_hbm.1, bf16[1,4096]{1,0:T(2,128)(2,1)} %reshape.17.gain_hbm, bf16[1,4096]{1,0:T(2,128)(2,1)} %reshape.18.weight_hbm, f32[2,256]{1,0:T(2,128)} %rewards_hbm.1, s32[2,256]{1,0:T(2,128)} %flags_hbm.1, ...), custom_call_target="tpu_custom_call" | custom-call | tf_op jit(solution)/shard_map/pallas_call | solution.py:321
  18.2 1.2 %copy.19 = f32[1,256]{1,0:T(1,128)} copy(f32[1,256]{1,0:T(1,128)} %get-tuple-element.16) | data formatting | bytes 2048
  19.4 1.2 %copy.20 = f32[1,256]{1,0:T(1,128)} copy(f32[1,256]{1,0:T(1,128)} %get-tuple-element.17) | data formatting | bytes 2048
  20.6 1.2 %copy.21 = f32[1,256]{1,0:T(1,128)} copy(f32[1,256]{1,0:T(1,128)} %get-tuple-element.18) | data formatting | bytes 2048

commit v2 on v1

--- a/solution.py
+++ b/solution.py
@@ -126,8 +126,8 @@
 
     for j in range(local_width // LANES):
         cols = pl.ds(j * LANES, LANES)
-        row = gain[0:1, cols].astype(jnp.float32) * wgt[0:1, cols].astype(jnp.float32)
-        scaled[:, cols] = jnp.broadcast_to(row, (8, LANES))
+        row = gain[cols].astype(jnp.float32) * wgt[cols].astype(jnp.float32)
+        scaled[:, cols] = jnp.broadcast_to(row.reshape(1, LANES), (8, LANES))
 
     lane = lax.broadcasted_iota(jnp.int32, (8, length), 1)
     steps = []
@@ -304,29 +304,36 @@
                 early[slots, r, length : 2 * length],
                 advs[t * own_rows + r] * scale,
             )
-    loss_ref[...] = total(sums) / count
+    loss_ref[...] = jnp.broadcast_to(total(sums) / count, (1, LANES))
 
     all_blocks(early, early_send_sem).wait()
     all_blocks(late, late_send_sem).wait()
 
 
-def shards(seq_count, tensor_count, hidden, norm_gain, value_weight, *rest):
-    seqs_all, length, local_width = hidden.shape
+def write_out(*refs):
+    half = len(refs) // 2
+    for src, dst in zip(refs[:half], refs[half:]):
+        dst[...] = src[:, : dst.shape[1]]
+
+
+def shards(seq_count, tensor_count, *args):
+    seqs_all, length, local_width = args[0].shape
     own_rows = seqs_all // tensor_count
     devices = seq_count * tensor_count
     chunk = min(length, 64)
     f32 = jnp.float32
     row = jax.ShapeDtypeStruct((own_rows, length), f32)
     dma = pltpu.SemaphoreType.DMA
+    shapes = [row, row, row, jax.ShapeDtypeStruct((1, 1), f32)]
     outs = pl.pallas_call(
         functools.partial(kernel, seq_count, tensor_count, local_width * tensor_count, chunk),
-        out_shape=[row, row, row, jax.ShapeDtypeStruct((1, 1), f32)],
-        in_specs=[pl.BlockSpec(memory_space=pl.ANY)] * 11,
+        out_shape=[row, row, row, jax.ShapeDtypeStruct((1, LANES), f32)],
+        in_specs=[pl.BlockSpec(memory_space=pltpu.HBM)] * 11,
         out_specs=[pl.BlockSpec(memory_space=pltpu.VMEM)] * 4,
         scratch_shapes=[
             pltpu.VMEM((seqs_all, length, local_width), jnp.bfloat16),
-            pltpu.VMEM((1, local_width), jnp.bfloat16),
-            pltpu.VMEM((1, local_width), jnp.bfloat16),
+            pltpu.VMEM((local_width,), jnp.bfloat16),
+            pltpu.VMEM((local_width,), jnp.bfloat16),
             pltpu.VMEM((seqs_all, length), f32),
             pltpu.VMEM((seqs_all, length), jnp.int32),
             pltpu.VMEM((own_rows, length), jnp.int32),
@@ -351,8 +358,17 @@
             dma,
             dma,
         ],
-        compiler_params=pltpu.CompilerParams(collective_id=0, has_side_effects=True),
-    )(hidden, norm_gain.reshape(1, -1), value_weight.reshape(1, -1), *rest)
+        compiler_params=pltpu.CompilerParams(
+            collective_id=0, has_side_effects=True, vmem_limit_bytes=24 << 20
+        ),
+    )(*[pltpu.with_memory_space_constraint(x, pltpu.HBM) for x in args])
+    outs = pl.pallas_call(
+        write_out,
+        out_shape=shapes,
+        in_specs=[pl.BlockSpec(memory_space=pltpu.VMEM)] * 4,
+        out_specs=[pl.BlockSpec(memory_space=pltpu.VMEM)] * 4,
+        compiler_params=pltpu.CompilerParams(vmem_limit_bytes=1 << 20),
+    )(*outs)
     return (outs[0], outs[1], outs[2], outs[3].reshape(()))
 
 

time: 23.9 us -> 15.8 us (0.66)
  local copies, waits for them, and re-layouts: 6.24 us -> 0 us
  between operations: 2.33 us -> 0.64 us
    unnamed x3 -> x0, local copies, waits for them, and re-layouts: 3.62 us -> none
    reshape x2 -> x0, local copies, waits for them, and re-layouts: 2.61 us -> none  [the longest x1 1.31 us: shards(): norm_gain.reshape(1, -1)]
    pallas_call x0 -> x1, Pallas kernels: none -> 0.58 us  [shards(): pl.pallas_call(write_out, out_shape=shapes, in_specs=[pl.BlockSpec(memory...]
    pallas_call x1, Pallas kernels: 14.9 us -> 14.4 us  [shards(): pl.pallas_call(functools.partial(kernel, seq_count, tensor_count, local_w...]
where the time goes in v2:
time: 15.8 us; the launch traced here: 15.6 us
  Pallas kernels  15 us (95%)
  between operations  0.64 us (4%)
    pallas_call x1, Pallas kernels, shards(): pl.pallas_call(functools.partial(kernel, seq_count, tensor_count, local_w...  14.4 us
    pallas_call x1, Pallas kernels, shards(): pl.pallas_call(write_out, out_shape=shapes, in_specs=[pl.BlockSpec(memory...  0.58 us

profile of v2, /device:TPU:0, one launch (start us, length us, event | category | flops | bytes accessed | tf_op | source)
XLA Modules:
  0.0 15.6 jit_solution(12433241863504128486)
XLA Ops:
  0.6 14.4 %shard_map.138 = (f32[1,256]{1,0:T(1,128)S(1)}, f32[1,256]{1,0:T(1,128)S(1)}, f32[1,256]{1,0:T(1,128)S(1)}, f32[1,128]{1,0:T(1,128)S(1)}) custom-call(bf16[2,256,4096]{2,1,0:T(8,128)(2,1)} %hidden_hbm.1, bf16[4096]{0:T(1024)(128)(2,1)} %gain_hbm.1, bf16[4096]{0:T(1024)(128)(2,1)} %weight_hbm.1, f32[2,256]{1,0:T(2,128)} %rewards_hbm.1, s32[2,256]{1,0:T(2,128)} %flags_hbm.1, ...), custom_call_target="tpu_custom_call" | custom-call | tf_op jit(solution)/shard_map/pallas_call | solution.py:328
  15.0 0.6 %shard_map.139 = (f32[1,256]{1,0:T(1,128)}, f32[1,256]{1,0:T(1,128)}, f32[1,256]{1,0:T(1,128)}, f32[1,1]{1,0:T(1,128)}) custom-call(f32[1,256]{1,0:T(1,128)S(1)} %get-tuple-element.12.refs_0_, f32[1,256]{1,0:T(1,128)S(1)} %get-tuple-element.13.refs_1_, f32[1,256]{1,0:T(1,128)S(1)} %get-tuple-element.14.refs_2_, f32[1,128]{1,0:T(1,128)S(1)} %get-tuple-element.15.refs_3_), custom_call_target="tpu_custom_call" | custom-call | tf_op jit(solution)/shard_map/pallas_call | solution.py:365

commit v3 on v2

--- a/solution.py
+++ b/solution.py
@@ -60,6 +60,7 @@
     early,
     late,
     carry,
+    slope,
     hid_sem,
     in_sem,
     part_send_sem,
@@ -98,7 +99,7 @@
 
     def hid_copy(i, c):
         row = lax.rem(first_row + own_rows + i, seqs_all)
-        rows = pl.ds(pl.multiple_of(c * chunk, chunk), chunk)
+        rows = pl.ds(c * chunk, chunk)
         return pltpu.make_async_copy(
             hidden_hbm.at[row, rows, :], hid.at[i, rows, :], hid_sem.at[i * chunks + c]
         )
@@ -137,36 +138,61 @@
         step *= 2
     ahead = lambda x, d: pltpu.roll(x, length - d, 1)
     rows_info = []
+    tasks = []
+
+    def scan_task(info, d):
+        def run():
+            info["levels"].append(info["level"])
+            info["level"] = info["level"] * ahead(info["level"], d)
+
+        return run
+
+    def coef_of(last_done, row):
+        shape = last_done.shape[:-1] + (length,)
+        at = lax.broadcasted_iota(jnp.int32, shape, len(shape) - 1).astype(jnp.float32)
+        discount = jnp.full(shape, disc[row], jnp.float32)
+        decay = discount * jnp.full(shape, trc[row], jnp.float32)
+        power = jnp.exp((length - 1.0 - at) * jnp.log(decay))
+        return jnp.where(at > last_done[..., 0:1], discount * power, 0.0)
+
     for r in range(own_rows):
         discount = jnp.full((8, length), disc[first_row + r], jnp.float32)
         trace = jnp.full((8, length), trc[first_row + r], jnp.float32)
         flags = jnp.broadcast_to(flg[pl.ds(first_row + r, 1), :], (8, length))
         alive = 1.0 - flags.astype(jnp.float32)
-        link = discount * trace * alive
-        level = jnp.where(lane < length - 1, link, 0.0)
-        coef = jnp.where(lane < length - 1, link, discount * alive)
-        levels = []
-        for d in steps:
-            levels.append(level)
-            level = level * ahead(level, d)
-            coef = coef * jnp.where(lane < length - d, ahead(coef, d), 1.0)
         ratio = jnp.exp(newp[r : r + 1, :] - oldp[r : r + 1, :])
         weight = msk[r : r + 1, :].astype(jnp.float32)
         reward = jnp.broadcast_to(rew[pl.ds(first_row + r, 1), :], (8, length))
-        following = jnp.where(lane < length - 1, discount * alive, 0.0)
-        rows_info.append((trace, levels, coef, ratio, weight, reward, following))
+        last_done = jnp.max(
+            jnp.where(flags > 0, lane, -1).astype(jnp.float32)[0:1, :], axis=1, keepdims=True
+        )
+        info = dict(
+            trace=trace,
+            level=jnp.where(lane < length - 1, discount * trace * alive, 0.0),
+            levels=[],
+            ratio=ratio,
+            weight=weight,
+            reward=reward,
+            following=jnp.where(lane < length - 1, discount * alive, 0.0),
+        )
+        rows_info.append(info)
+        tasks += [scan_task(info, d) for d in steps]
         early[my_slot, r : r + 1, 0:length] = ratio
         early[my_slot, r : r + 1, length : 2 * length] = weight
-        early[my_slot, r : r + 1, 2 * length : 3 * length] = coef[0:1, :]
-        early[my_slot, r : r + 1, 3 * length : 3 * length + LANES] = jnp.broadcast_to(
-            trace[0:1, 0:1] * coef[0:1, 0:1], (1, LANES)
-        )
+        early[my_slot, r : r + 1, 2 * length : 2 * length + LANES] = jnp.broadcast_to(
+            last_done, (1, LANES)
+        )
+    all_chunks = seqs_all * chunks
+    task_count = len(tasks)
 
     def row_sums(i):
-        def do_chunk(c, _):
+        for c in range(chunks):
+            g = i * chunks + c
             hid_copy(i, c).wait()
+            for task in tasks[g * task_count // all_chunks : (g + 1) * task_count // all_chunks]:
+                task()
             for b in range(chunk // BLOCK):
-                rows = pl.ds(pl.multiple_of(c * chunk + b * BLOCK, BLOCK), BLOCK)
+                rows = pl.ds(c * chunk + b * BLOCK, BLOCK)
                 squares = jnp.zeros((BLOCK // 8, 8, LANES), jnp.float32)
                 products = jnp.zeros((BLOCK // 8, 8, LANES), jnp.float32)
                 for j in range(local_width // LANES):
@@ -176,9 +202,6 @@
                     products = products + x * scaled[:, cols][None]
                 parts[0, rows, :] = squares.reshape(BLOCK, LANES)
                 parts[1, rows, :] = products.reshape(BLOCK, LANES)
-            return 0
-
-        lax.fori_loop(0, chunks, do_chunk, 0)
         return lane_sums(parts[0]), lane_sums(parts[1])
 
     for k in range(1, tensor_count):
@@ -227,7 +250,10 @@
         copy.wait()
 
     for r in range(own_rows):
-        trace, levels, coef, ratio, weight, reward, following = rows_info[r]
+        info = rows_info[r]
+        trace, levels, reward, following = (
+            info[name] for name in ("trace", "levels", "reward", "following")
+        )
         squares, products = own[r]
         for k in range(1, tensor_count):
             squares = squares + part_recv[k - 1, 2 * r : 2 * r + 1, :]
@@ -251,6 +277,14 @@
             count = count + early[pl.ds(t * seq_count, seq_count), r, length : 2 * length]
     total = lambda x: jnp.sum(jnp.sum(x, axis=0, keepdims=True), axis=1, keepdims=True)
     count = total(count)
+    coefs = []
+    for t in range(tensor_count):
+        for r in range(own_rows):
+            row = t * own_rows + r
+            slots = pl.ds(t * seq_count, seq_count)
+            coef = coef_of(early[slots, r, 2 * length : 2 * length + LANES], row)
+            coefs.append(coef)
+            slope[slots, r, :] = jnp.broadcast_to(trc[row] * coef[:, 0:1], (seq_count, LANES))
     all_blocks(late, late_recv_sem).wait()
 
     advs = []
@@ -262,14 +296,13 @@
                 carry[slot, r : r + 1, :] = entering
                 if n:
                     offset = late[slot, r : r + 1, length : length + LANES]
-                    slope = early[slot, r : r + 1, 3 * length : 3 * length + LANES]
-                    entering = offset + slope * entering
+                    entering = offset + slope[slot, r : r + 1, :] * entering
     sums = jnp.zeros((seq_count, length), jnp.float32)
     for t in range(tensor_count):
         for r in range(own_rows):
             slots = pl.ds(t * seq_count, seq_count)
             entering = jnp.concatenate([carry[slots, r, :]] * (length // LANES), axis=1)
-            adv = late[slots, r, 0:length] + early[slots, r, 2 * length : 3 * length] * entering
+            adv = late[slots, r, 0:length] + coefs[t * own_rows + r] * entering
             advs.append(adv)
             sums = sums + early[slots, r, length : 2 * length] * adv
     mean = total(sums) / count
@@ -287,10 +320,11 @@
         return -weight * jnp.minimum(ratio * white, clipped * white)
 
     for r in range(own_rows):
-        _, _, coef, ratio, weight, _, _ = rows_info[r]
+        ratio, weight = rows_info[r]["ratio"], rows_info[r]["weight"]
+        coef = coef_of(early[my_slot, r : r + 1, 2 * length : 2 * length + LANES], first_row + r)
         entering = carry[my_slot, r : r + 1, :]
         entering = jnp.concatenate([entering] * (length // LANES), axis=1)
-        adv = late[my_slot, r : r + 1, 0:length] + coef[0:1, :] * entering
+        adv = late[my_slot, r : r + 1, 0:length] + coef * entering
         white = (adv - mean) * scale
         white_ref[r : r + 1, :] = white
         token_ref[r : r + 1, :] = token_loss(ratio, weight, white)
@@ -346,8 +380,9 @@
             pltpu.VMEM((2, length, LANES), f32),
             pltpu.VMEM((max(tensor_count - 1, 1), 2 * own_rows, length), f32),
             pltpu.VMEM((max(tensor_count - 1, 1), 2 * own_rows, length), f32),
-            pltpu.VMEM((devices, own_rows, 3 * length + LANES), f32),
+            pltpu.VMEM((devices, own_rows, 2 * length + LANES), f32),
             pltpu.VMEM((devices, own_rows, length + LANES), f32),
+            pltpu.VMEM((devices, own_rows, LANES), f32),
             pltpu.VMEM((devices, own_rows, LANES), f32),
             dma((seqs_all * (length // chunk),)),
             dma((10,)),

time: 15.8 us -> 15.2 us (0.962)
  Pallas kernels: 15 us -> 14.4 us
    pallas_call x1, Pallas kernels: 14.4 us -> 13.8 us  [shards(): pl.pallas_call(functools.partial(kernel, seq_count, tensor_count, local_w...]
where the time goes in v3:
time: 15.2 us; the launch traced here: 15 us
  Pallas kernels  14.4 us (95%)
  between operations  0.64 us (4%)
    pallas_call x1, Pallas kernels, shards(): pl.pallas_call(functools.partial(kernel, seq_count, tensor_count, local_w...  13.8 us
    pallas_call x1, Pallas kernels, shards(): pl.pallas_call(write_out, out_shape=shapes, in_specs=[pl.BlockSpec(memory...  0.58 us

profile of v3, /device:TPU:0, one launch (start us, length us, event | category | flops | bytes accessed | tf_op | source)
XLA Modules:
  0.0 15.0 jit_solution(16237627199579470990)
XLA Ops:
  0.6 13.8 %shard_map.138 = (f32[1,256]{1,0:T(1,128)S(1)}, f32[1,256]{1,0:T(1,128)S(1)}, f32[1,256]{1,0:T(1,128)S(1)}, f32[1,128]{1,0:T(1,128)S(1)}) custom-call(bf16[2,256,4096]{2,1,0:T(8,128)(2,1)} %hidden_hbm.1, bf16[4096]{0:T(1024)(128)(2,1)} %gain_hbm.1, bf16[4096]{0:T(1024)(128)(2,1)} %weight_hbm.1, f32[2,256]{1,0:T(2,128)} %rewards_hbm.1, s32[2,256]{1,0:T(2,128)} %flags_hbm.1, ...), custom_call_target="tpu_custom_call" | custom-call | tf_op jit(solution)/shard_map/pallas_call | solution.py:362
  14.4 0.6 %shard_map.139 = (f32[1,256]{1,0:T(1,128)}, f32[1,256]{1,0:T(1,128)}, f32[1,256]{1,0:T(1,128)}, f32[1,1]{1,0:T(1,128)}) custom-call(f32[1,256]{1,0:T(1,128)S(1)} %get-tuple-element.12.refs_0_, f32[1,256]{1,0:T(1,128)S(1)} %get-tuple-element.13.refs_1_, f32[1,256]{1,0:T(1,128)S(1)} %get-tuple-element.14.refs_2_, f32[1,128]{1,0:T(1,128)S(1)} %get-tuple-element.15.refs_3_), custom_call_target="tpu_custom_call" | custom-call | tf_op jit(solution)/shard_map/pallas_call | solution.py:400

commit v4 on v3

--- a/solution.py
+++ b/solution.py
@@ -10,16 +10,23 @@
 EPS_NORM = 1e-06
 EPS_WHITE = 1e-08
 CLIP = 0.2
-HIGHEST = lax.Precision.HIGHEST
 LANES = 128
 BLOCK = 32
+UNROLLED = 64
 
 
 def lane_sums(parts):
-    ones = jnp.ones((8, LANES), jnp.float32)
-    return lax.dot_general(
-        ones, parts, (((1,), (1,)), ((), ())), precision=HIGHEST, preferred_element_type=jnp.float32
-    )
+    total = 0.0
+    for _ in range(3):
+        piece = parts.astype(jnp.bfloat16)
+        parts = parts - piece.astype(jnp.float32)
+        total = total + lax.dot_general(
+            jnp.ones((8, LANES), jnp.bfloat16),
+            piece,
+            (((1,), (1,)), ((), ())),
+            preferred_element_type=jnp.float32,
+        )
+    return total
 
 
 def kernel(
@@ -114,13 +121,20 @@
         slot = lax.rem(my_slot + k, devices)
         return (lax.rem(slot, seq_count), lax.div(slot, seq_count))
 
+    def each_peer(act):
+        if devices <= UNROLLED:
+            for k in range(1, devices):
+                act(k, 0)
+        else:
+            lax.fori_loop(1, devices, act, 0)
+
     def greet(k, _):
         pl.semaphore_signal(
             barrier, inc=1, device_id=peer(k), device_id_type=pl.DeviceIdType.MESH
         )
         return 0
 
-    lax.fori_loop(1, devices, greet, 0)
+    each_peer(greet)
 
     for copy in small_copies:
         copy.wait()
@@ -135,15 +149,17 @@
     step = 1
     while step < length:
         steps.append(step)
-        step *= 2
-    ahead = lambda x, d: pltpu.roll(x, length - d, 1)
+        step *= 4
+    ahead = lambda x, d: pltpu.roll(x, (length - d) % length, 1)
     rows_info = []
     tasks = []
 
     def scan_task(info, d):
         def run():
-            info["levels"].append(info["level"])
-            info["level"] = info["level"] * ahead(info["level"], d)
+            one = info["level"]
+            two = one * ahead(one, d)
+            info["levels"] += [(d, one), (2 * d, two), (3 * d, one * ahead(two, d))]
+            info["level"] = two * ahead(two, 2 * d)
 
         return run
 
@@ -186,6 +202,7 @@
     task_count = len(tasks)
 
     def row_sums(i):
+        start, squares_rows, products_rows = 0, [], []
         for c in range(chunks):
             g = i * chunks + c
             hid_copy(i, c).wait()
@@ -202,7 +219,13 @@
                     products = products + x * scaled[:, cols][None]
                 parts[0, rows, :] = squares.reshape(BLOCK, LANES)
                 parts[1, rows, :] = products.reshape(BLOCK, LANES)
-        return lane_sums(parts[0]), lane_sums(parts[1])
+            done = (c + 1) * chunk
+            if done % LANES == 0 or done == length:
+                rows = pl.ds(start, done - start)
+                squares_rows.append(lane_sums(parts[0, rows, :]))
+                products_rows.append(lane_sums(parts[1, rows, :]))
+                start = done
+        return jnp.concatenate(squares_rows, axis=1), jnp.concatenate(products_rows, axis=1)
 
     for k in range(1, tensor_count):
         for r in range(own_rows):
@@ -237,7 +260,7 @@
             ).start()
             return 0
 
-        lax.fori_loop(1, devices, send, 0)
+        each_peer(send)
 
     def all_blocks(buffer, sem):
         view = buffer.at[pl.ds(0, devices - 1)]
@@ -261,8 +284,8 @@
         values = products * lax.rsqrt(squares / width + EPS_NORM)
         values_ref[r : r + 1, :] = values[0:1, :]
         adv = reward + following * ahead(values, 1) - values
-        for d, level in zip(steps, levels):
-            adv = adv + level * ahead(adv, d)
+        for n in range(0, len(levels), 3):
+            adv = adv + sum(level * ahead(adv, d) for d, level in levels[n : n + 3] if d < length)
         late[my_slot, r : r + 1, 0:length] = adv[0:1, :]
         late[my_slot, r : r + 1, length : length + LANES] = jnp.broadcast_to(
             values[0:1, 0:1] + trace[0:1, 0:1] * adv[0:1, 0:1], (1, LANES)

time: 15.2 us -> 15 us (0.987)
  Pallas kernels: 14.4 us -> 14.1 us
    pallas_call x1, Pallas kernels: 13.8 us -> 13.5 us  [shards(): pl.pallas_call(functools.partial(kernel, seq_count, tensor_count, local_w...]
where the time goes in v4:
time: 15 us; the launch traced here: 14.7 us
  Pallas kernels  14.1 us (94%)
  between operations  0.64 us (4%)
    pallas_call x1, Pallas kernels, shards(): pl.pallas_call(functools.partial(kernel, seq_count, tensor_count, local_w...  13.5 us
    pallas_call x1, Pallas kernels, shards(): pl.pallas_call(write_out, out_shape=shapes, in_specs=[pl.BlockSpec(memory...  0.58 us

profile of v4, /device:TPU:0, one launch (start us, length us, event | category | flops | bytes accessed | tf_op | source)
XLA Modules:
  0.0 14.7 jit_solution(4380272100346012154)
XLA Ops:
  0.6 13.5 %shard_map.138 = (f32[1,256]{1,0:T(1,128)S(1)}, f32[1,256]{1,0:T(1,128)S(1)}, f32[1,256]{1,0:T(1,128)S(1)}, f32[1,128]{1,0:T(1,128)S(1)}) custom-call(bf16[2,256,4096]{2,1,0:T(8,128)(2,1)} %hidden_hbm.1, bf16[4096]{0:T(1024)(128)(2,1)} %gain_hbm.1, bf16[4096]{0:T(1024)(128)(2,1)} %weight_hbm.1, f32[2,256]{1,0:T(2,128)} %rewards_hbm.1, s32[2,256]{1,0:T(2,128)} %flags_hbm.1, ...), custom_call_target="tpu_custom_call" | custom-call | tf_op jit(solution)/shard_map/pallas_call | solution.py:385
  14.2 0.6 %shard_map.139 = (f32[1,256]{1,0:T(1,128)}, f32[1,256]{1,0:T(1,128)}, f32[1,256]{1,0:T(1,128)}, f32[1,1]{1,0:T(1,128)}) custom-call(f32[1,256]{1,0:T(1,128)S(1)} %get-tuple-element.12.refs_0_, f32[1,256]{1,0:T(1,128)S(1)} %get-tuple-element.13.refs_1_, f32[1,256]{1,0:T(1,128)S(1)} %get-tuple-element.14.refs_2_, f32[1,128]{1,0:T(1,128)S(1)} %get-tuple-element.15.refs_3_), custom_call_target="tpu_custom_call" | custom-call | tf_op jit(solution)/shard_map/pallas_call | solution.py:423

commit v5 on v4

--- a/solution.py
+++ b/solution.py
@@ -13,6 +13,7 @@
 LANES = 128
 BLOCK = 32
 UNROLLED = 64
+IN_FLIGHT = 4
 
 
 def lane_sums(parts):
@@ -111,9 +112,8 @@
             hidden_hbm.at[row, rows, :], hid.at[i, rows, :], hid_sem.at[i * chunks + c]
         )
 
-    for i in range(seqs_all):
-        for c in range(chunks):
-            hid_copy(i, c).start()
+    for g in range(min(IN_FLIGHT, seqs_all * chunks)):
+        hid_copy(g // chunks, g % chunks).start()
 
     barrier = pltpu.get_barrier_semaphore()
 
@@ -206,6 +206,8 @@
         for c in range(chunks):
             g = i * chunks + c
             hid_copy(i, c).wait()
+            if g + IN_FLIGHT < all_chunks:
+                hid_copy((g + IN_FLIGHT) // chunks, (g + IN_FLIGHT) % chunks).start()
             for task in tasks[g * task_count // all_chunks : (g + 1) * task_count // all_chunks]:
                 task()
             for b in range(chunk // BLOCK):

time: 15 us -> 14.6 us (0.973)
  Pallas kernels: 14.1 us -> 13.7 us
    pallas_call x1, Pallas kernels: 13.5 us -> 13.1 us  [shards(): pl.pallas_call(functools.partial(kernel, seq_count, tensor_count, local_w...]
where the time goes in v5:
time: 14.6 us; the launch traced here: 14.4 us
  Pallas kernels  13.7 us (94%)
  between operations  0.64 us (4%)
    pallas_call x1, Pallas kernels, shards(): pl.pallas_call(functools.partial(kernel, seq_count, tensor_count, local_w...  13.1 us
    pallas_call x1, Pallas kernels, shards(): pl.pallas_call(write_out, out_shape=shapes, in_specs=[pl.BlockSpec(memory...  0.58 us

profile of v5, /device:TPU:0, one launch (start us, length us, event | category | flops | bytes accessed | tf_op | source)
XLA Modules:
  0.0 14.4 jit_solution(5140261610321761891)
XLA Ops:
  0.6 13.1 %shard_map.138 = (f32[1,256]{1,0:T(1,128)S(1)}, f32[1,256]{1,0:T(1,128)S(1)}, f32[1,256]{1,0:T(1,128)S(1)}, f32[1,128]{1,0:T(1,128)S(1)}) custom-call(bf16[2,256,4096]{2,1,0:T(8,128)(2,1)} %hidden_hbm.1, bf16[4096]{0:T(1024)(128)(2,1)} %gain_hbm.1, bf16[4096]{0:T(1024)(128)(2,1)} %weight_hbm.1, f32[2,256]{1,0:T(2,128)} %rewards_hbm.1, s32[2,256]{1,0:T(2,128)} %flags_hbm.1, ...), custom_call_target="tpu_custom_call" | custom-call | tf_op jit(solution)/shard_map/pallas_call | solution.py:387
  13.8 0.6 %shard_map.139 = (f32[1,256]{1,0:T(1,128)}, f32[1,256]{1,0:T(1,128)}, f32[1,256]{1,0:T(1,128)}, f32[1,1]{1,0:T(1,128)}) custom-call(f32[1,256]{1,0:T(1,128)S(1)} %get-tuple-element.12.refs_0_, f32[1,256]{1,0:T(1,128)S(1)} %get-tuple-element.13.refs_1_, f32[1,256]{1,0:T(1,128)S(1)} %get-tuple-element.14.refs_2_, f32[1,128]{1,0:T(1,128)S(1)} %get-tuple-element.15.refs_3_), custom_call_target="tpu_custom_call" | custom-call | tf_op jit(solution)/shard_map/pallas_call | solution.py:425
